TPU v7x, 256 devices: a whole 4x4x8 slice. The times are simulated.
256 devices in a mesh: ops: 64 (over x, z, core), sec: 4 (over y).
Axes of the slice: x: 4, y: 4, z: 8, core: 2. Of those that a mesh axis runs over, the one named last changes fastest.
Arguments:
- operators: bfloat16 [128, 8, 768, 768], P('ops', 'sec'), may hold values from -6 to 6
- basis: bfloat16 [8, 768, 768], P('sec'), may hold values from -0.21875 to 0.21875
- shift: int32 [128], replicated, may hold values from -1 to 1
- dest: int32 [128], replicated, may hold values from 0 to 127, each once
- sector_sizes: int32 [8], replicated, may hold values from 384 to 768
Outputs:
- renormalized: bfloat16 [128, 8, 768, 768], P('ops', 'sec')
Inputs may be any that keep to these rules, and one draw needn't show every extreme that they name: `shift`: each pair's offset is -1, 0 or 1. dest names every index of 0 to 127 once.
All inputs are finite; a program needn't handle non-finite values.
Results may differ from a plain program's by a relative error of at most 0.0049.
Values may be sent and summed in bfloat16 or wider, within the bound.
A program may use at most 128 MiB of HBM per device.

v0:
```python
import jax
import jax.numpy as jnp
from jax import lax
from jax.sharding import PartitionSpec as P


def with_halo(block, sides, width):
    for axis, dim in sides:
        count = lax.axis_size(axis)
        forward = [(i, i + 1) for i in range(count - 1)]
        forward.append((count - 1, 0))
        backward = [(target, source) for source, target in forward]
        low = lax.ppermute(
            lax.slice_in_dim(block, block.shape[dim] - width, None, axis=dim), axis, forward
        )
        high = lax.ppermute(lax.slice_in_dim(block, 0, width, axis=dim), axis, backward)
        block = jnp.concatenate([low, block, high], axis=dim)
    return block


def body(operators, basis, shift, dest, sector_sizes):
    pair_dev = operators.shape[0]
    sector_dev = operators.shape[1]
    width = operators.shape[3]
    ops_count = lax.axis_size("ops")
    total_sectors = sector_dev * lax.axis_size("sec")
    sector_pos = lax.axis_index("sec")
    ops_pos = lax.axis_index("ops")
    nearby = with_halo(basis, (("sec", 0),), 1)
    near_ids = (
        sector_pos * sector_dev - 1 + jnp.arange(sector_dev + 2, dtype=jnp.int32)
    ) % total_sectors
    own_local = jnp.arange(sector_dev, dtype=jnp.int32) + 1
    columns = jnp.arange(width, dtype=jnp.int32)
    near_sizes = jnp.take(sector_sizes, near_ids)
    kept = columns[None, :] < near_sizes[:, None]
    kept_near = jnp.where(kept[:, None, :], nearby, jnp.zeros_like(nearby))
    own_basis = jnp.take(kept_near, own_local, axis=0)
    source = jnp.argsort(dest, stable=True)
    mine = lax.dynamic_slice_in_dim(source, ops_pos * pair_dev, pair_dev)
    offsets = jnp.take(shift, mine)
    strip = width // ops_count
    split = operators.reshape(pair_dev, sector_dev, ops_count, strip, width)
    spread = lax.all_to_all(split, "ops", split_axis=2, concat_axis=0, tiled=True)
    ordered = jnp.take(spread, source, axis=0)
    returned = lax.all_to_all(ordered, "ops", split_axis=0, concat_axis=2, tiled=True)
    blocks = returned.reshape(pair_dev, sector_dev, width, width)
    target_local = own_local[None, :] + offsets[:, None]
    half = jnp.einsum(
        "psab,sbc->psac", blocks, own_basis, preferred_element_type=jnp.float32
    ).astype(jnp.bfloat16)
    targets = jnp.take(kept_near, target_local.reshape(-1), axis=0)
    targets = targets.reshape(blocks.shape[0], sector_dev, width, width)
    return jnp.einsum("psba,psbc->psac", targets, half, preferred_element_type=jnp.float32).astype(
        jnp.bfloat16
    )


def solution(mesh):
    return jax.shard_map(
        body,
        mesh=mesh,
        in_specs=(P("ops", "sec", None, None), P("sec", None, None), P(), P(), P()),
        out_specs=P("ops", "sec", None, None),
        check_vma=False,
    )
```

profile of v0, /device:TPU:1, one launch (start us, length us, event | category | flops | bytes accessed | tf_op | source)
XLA Modules:
  0.0 295.1 jit_solution(11162149202697768702)
XLA Ops:
  0.0 0.0 copy-start
  0.0 9.4 %copy.12 = bf16[2,2,768,768]{3,1,2,0:T(2,128)(2,1)} copy(bf16[2,2,768,768]{3,2,1,0:T(8,128)(2,1)} %param.5) | data formatting | bytes 9437184 | tf_op args[0]
  9.4 7.7 %copy.13 = bf16[2,2,64,12,768]{4,1,3,0,2:T(2,128)(2,1)} copy(bf16[2,2,64,12,768]{4,1,3,2,0:T(2,128)(2,1)} %bitcast.33) | data formatting | bytes 9437184 | tf_op jit(solution)/shard_map/reshape | solution.py:43
  17.1 0.0 copy-start.5
  17.1 13.3 %all-to-all-start = ((bf16[2,2,64,12,768]{4,1,3,0,2:T(2,128)(2,1)}), bf16[2,2,64,12,768]{4,1,3,0,2:T(2,128)(2,1)}, u32[]{:S(2)}, u32[]{:S(2)}) async-start(bf16[2,2,64,12,768]{4,1,3,0,2:T(2,128)(2,1)} %copy.13), calls=%async_computation | async-start | bytes 9437184 | tf_op jit(solution)/shard_map/all_to_all | solution.py:44
  30.4 0.0 copy-done.5
  30.5 2.5 sort.17
  33.0 0.0 copy-start.4
  33.0 104.5 %all-to-all-done = bf16[2,2,64,12,768]{4,1,3,0,2:T(2,128)(2,1)} async-done(((bf16[2,2,64,12,768]{4,1,3,0,2:T(2,128)(2,1)}), bf16[2,2,64,12,768]{4,1,3,0,2:T(2,128)(2,1)}, u32[]{:S(2)}, u32[]{:S(2)}) %all-to-all-start) | async-done | bytes 4718624 | tf_op jit(solution)/shard_map/all_to_all | solution.py:44
  137.5 15.6 %gather_fusion.4 = bf16[128,2,12,768]{3,1,2,0:T(2,128)(2,1)} fusion(bf16[128,2,12,768]{3,1,2,0:T(2,128)(2,1)} %bitcast.8, s32[1024]{0:T(1024)S(1)} %pad_clamp_fusion), kind=kCustom, calls=%fused_computation.4 | custom fusion | bytes 9437696 | tf_op jit(solution)/shard_map/jit(_take)/gather | solution.py:45
  153.1 8.8 %fusion.6 = bf16[128,2,1,12,768]{4,1,3,2,0:T(2,128)(2,1)} fusion(bf16[128,2,12,768]{3,1,2,0:T(2,128)(2,1)} %gather_fusion.4, pred[128]{0:T(512)(128)(4,1)S(1)} %compare_and_fusion), kind=kLoop, calls=%fused_computation.13 | loop fusion | flops 2359296 | bytes 9437312 | tf_op jit(solution)/shard_map/jit(_take)/select_n | solution.py:45
  161.9 0.0 copy-start.2
  161.9 6.1 %all-to-all-start.1 = ((bf16[128,2,1,12,768]{4,1,3,2,0:T(2,128)(2,1)}), bf16[128,2,1,12,768]{4,1,3,2,0:T(2,128)(2,1)}, u32[]{:S(2)}, u32[]{:S(2)}) async-start(bf16[128,2,1,12,768]{4,1,3,2,0:T(2,128)(2,1)} %fusion.6), calls=%async_computation.1 | async-start | bytes 9437184 | tf_op jit(solution)/shard_map/all_to_all | solution.py:46
  168.0 0.0 copy-done.2
  168.1 0.0 copy-start.1
  168.1 1.6 fusion.33
  169.6 1.3 collective-permute-start
  170.9 1.4 collective-permute-start.1
  172.4 0.0 copy-done.4
  172.4 0.1 compare_select_fusion.7
  172.5 0.0 copy-done.1
  172.5 1.2 gather_fusion
  173.6 0.7 and_select_fusion.3
  174.3 0.0 copy-start.3
  174.3 0.1 broadcast_add_fusion
  174.4 0.7 add.175
  175.1 0.0 copy-done
  175.1 1.2 gather_fusion.1
  176.3 0.5 compare_and_fusion.1
  176.8 0.7 fusion.30
  177.5 0.0 copy-done.3
  177.5 0.7 and_select_fusion.1
  178.2 1.3 compare_and_fusion.2
  179.4 0.1 iota_compare_fusion
  179.5 18.7 %collective-permute-done = bf16[1,768,768]{2,1,0:T(8,128)(2,1)S(1)} collective-permute-done((bf16[1,768,768]{2,1,0:T(8,128)(2,1)}, bf16[1,768,768]{2,1,0:T(8,128)(2,1)S(1)}, u32[]{:S(2)}, u32[]{:S(2)}) %collective-permute-start) | collective-permute-done | bytes 1179680 | tf_op jit(solution)/shard_map/ppermute | solution.py:13
  198.2 0.0 collective-permute-done.1
  198.2 3.7 %maximum_select_fusion = bf16[4,768,768]{2,1,0:T(8,128)(2,1)} fusion(bf16[1,768,768]{2,1,0:T(8,128)(2,1)} %collective-permute-done.1, bf16[2,768,768]{2,1,0:T(8,128)(2,1)S(1)} %copy-done.2, bf16[1,768,768]{2,1,0:T(8,128)(2,1)S(1)} %collective-permute-done, pred[4,768]{1,0:T(4,128)(4,1)S(1)} %iota_compare_fusion), kind=kLoop, calls=%fused_computation.6 | loop fusion | flops 7077888 | bytes 9440256 | tf_op jit(solution)/shard_map/jit(_where)/select_n | solution.py:37
  201.9 5.3 %gather_fusion.2 = bf16[4,768,768]{2,1,0:T(8,128)(2,1)} fusion(bf16[4,768,768]{2,1,0:T(8,128)(2,1)} %maximum_select_fusion, s32[1024]{0:T(1024)S(1)} %pad_clamp_fusion.2), kind=kCustom, calls=%fused_computation.2 | custom fusion | bytes 9437200 | tf_op jit(solution)/shard_map/jit(_take)/gather | solution.py:52
  207.2 6.6 %copy.11 = bf16[2,2,768,768]{2,3,1,0:T(8,128)(2,1)} copy(bf16[2,2,768,768]{3,2,1,0:T(8,128)(2,1)} %bitcast.32) | data formatting | bytes 9437184 | tf_op jit(solution)/shard_map/jit(_take)/gather | solution.py:52
  213.8 3.0 %gather_fusion.3 = bf16[2,768,768]{2,1,0:T(8,128)(2,1)S(1)} fusion(bf16[4,768,768]{2,1,0:T(8,128)(2,1)} %maximum_select_fusion, s32[1024]{0:T(1024)S(1)} %pad_clamp_fusion.1), kind=kCustom, calls=%fused_computation.3 | custom fusion | bytes 4718600 | tf_op jit(solution)/shard_map/jit(_take)/gather | solution.py:38
  216.9 58.3 %all-to-all-done.1 = bf16[128,2,1,12,768]{4,1,3,2,0:T(2,128)(2,1)} async-done(((bf16[128,2,1,12,768]{4,1,3,2,0:T(2,128)(2,1)}), bf16[128,2,1,12,768]{4,1,3,2,0:T(2,128)(2,1)}, u32[]{:S(2)}, u32[]{:S(2)}) %all-to-all-start.1) | async-done | bytes 4718624 | tf_op jit(solution)/shard_map/all_to_all | solution.py:46
  275.2 0.0 copy-start.6
  275.2 0.0 copy-start.7
  275.2 7.8 %copy.15 = bf16[64,2,2,1,12,768]{5,2,4,0,1,3:T(2,128)(2,1)} copy(bf16[64,2,2,1,12,768]{5,2,4,1,0,3:T(2,128)(2,1)} %bitcast.11) | data formatting | bytes 9437184 | tf_op jit(solution)/shard_map/all_to_all | solution.py:46
  282.9 0.0 copy-done.6
  282.9 0.0 copy-done.7
  282.9 12.2 %fusion.8 = bf16[2,2,768,768]{3,2,1,0:T(8,128)(2,1)} fusion(bf16[2,2,768,768]{2,3,1,0:T(8,128)(2,1)} %copy.11, pred[2,2]{1,0:T(4,128)(4,1)S(1)} %copy-done.6, bf16[2,2,768,768]{3,1,2,0:T(2,128)(2,1)} %bitcast.34, bf16[2,768,768]{2,1,0:T(8,128)(2,1)S(1)} %gather_fusion.3, pred[2]{0:T(512)(128)(4,1)S(1)} %copy-done.7), kind=kOutput, calls=%fused_computation.15 | convolution fusion | flops 7256014848 | bytes 16515078 | tf_op jit(solution)/shard_map/psba,psbc->psac/dot_general | solution.py:54
  (10 shorter events, 0.1 us)
Async XLA Ops:
  0.0 175.1 %copy-start = (s32[8]{0:T(128)S(1)}, s32[8]{0:T(128)}, u32[]{:S(2)}) copy-start(s32[8]{0:T(128)} %param.9) | copy-start | bytes 100
  17.1 13.3 %copy-start.5 = (s32[128]{0:T(128)S(1)}, s32[128]{0:T(128)}, u32[]{:S(2)}) copy-start(s32[128]{0:T(128)} %param.8) | copy-start | bytes 1540
  17.1 120.4 %all-to-all-start = ((bf16[2,2,64,12,768]{4,1,3,0,2:T(2,128)(2,1)}), bf16[2,2,64,12,768]{4,1,3,0,2:T(2,128)(2,1)}, u32[]{:S(2)}, u32[]{:S(2)}) async-start(bf16[2,2,64,12,768]{4,1,3,0,2:T(2,128)(2,1)} %copy.13), calls=%async_computation | async-start | bytes 9437184 | tf_op jit(solution)/shard_map/all_to_all | solution.py:44
  33.0 139.4 %copy-start.4 = (s32[128]{0:T(128)}, s32[128]{0:T(128)S(1)}, u32[]{:S(2)}) copy-start(s32[128]{0:T(128)S(1)} %get-tuple-element.6) | copy-start | bytes 1540
  161.9 6.1 %copy-start.2 = (bf16[2,768,768]{2,1,0:T(8,128)(2,1)S(1)}, bf16[2,768,768]{2,1,0:T(8,128)(2,1)}, u32[]{:S(2)}) copy-start(bf16[2,768,768]{2,1,0:T(8,128)(2,1)} %param.6) | copy-start | bytes 7077892
  161.9 113.3 %all-to-all-start.1 = ((bf16[128,2,1,12,768]{4,1,3,2,0:T(2,128)(2,1)}), bf16[128,2,1,12,768]{4,1,3,2,0:T(2,128)(2,1)}, u32[]{:S(2)}, u32[]{:S(2)}) async-start(bf16[128,2,1,12,768]{4,1,3,2,0:T(2,128)(2,1)} %fusion.6), calls=%async_computation.1 | async-start | bytes 9437184 | tf_op jit(solution)/shard_map/all_to_all | solution.py:46
  168.1 4.4 %copy-start.1 = (s32[128]{0:T(128)S(1)}, s32[128]{0:T(128)}, u32[]{:S(2)}) copy-start(s32[128]{0:T(128)} %param.7) | copy-start | bytes 1540
  169.6 28.6 %collective-permute-start = (bf16[1,768,768]{2,1,0:T(8,128)(2,1)}, bf16[1,768,768]{2,1,0:T(8,128)(2,1)S(1)}, u32[]{:S(2)}, u32[]{:S(2)}) collective-permute-start(bf16[1,768,768]{2,1,0:T(8,128)(2,1)} %get-tuple-element.7), channel_id=1, source_target_pairs={{0,1},{1,2},{2,3},{3,0},{4,5},{5,6},{6,7},{7,4},{8,9},{9,10},{10,1... | collective-permute-start | bytes 3538952 | tf_op jit(solution)/shard_map/ppermute | solution.py:13
  170.9 27.3 %collective-permute-start.1 = (bf16[1,768,768]{2,1,0:T(8,128)(2,1)}, bf16[1,768,768]{2,1,0:T(8,128)(2,1)}, u32[]{:S(2)}, u32[]{:S(2)}) collective-permute-start(bf16[1,768,768]{2,1,0:T(8,128)(2,1)} %get-tuple-element.8), channel_id=1, source_target_pairs={{1,0},{2,1},{3,2},{0,3},{5,4},{6,5},{7,6},{4,7},{9,8},{10,9},{11,1... | collective-permute-start | bytes 3538952 | tf_op jit(solution)/shard_map/ppermute | solution.py:16
  174.3 3.2 %copy-start.3 = (s32[2]{0:T(128)}, s32[2]{0:T(128)S(1)}, u32[]{:S(2)}) copy-start(s32[2]{0:T(128)S(1)} %get-tuple-element.10) | copy-start | bytes 28
  275.2 7.8 %copy-start.6 = (pred[2,2]{1,0:T(4,128)(4,1)S(1)}, pred[2,2]{1,0:T(4,128)(4,1)}, u32[]{:S(2)}) copy-start(pred[2,2]{1,0:T(4,128)(4,1)} %compare_and_fusion.2) | copy-start | bytes 16
  275.2 7.8 %copy-start.7 = (pred[2]{0:T(512)(128)(4,1)S(1)}, pred[2]{0:T(512)(128)(4,1)}, u32[]{:S(2)}) copy-start(pred[2]{0:T(512)(128)(4,1)} %compare_and_fusion.1) | copy-start | bytes 10
where the time goes:
time: 296 us; the launch traced here: 295 us
  waiting for transfers between devices  181 us (61%)
  local copies, waits for them, and re-layouts  60.1 us (20%)
  starting transfers between devices  22.2 us (8%)
  other arithmetic  19.1 us (6%)
  matrix products  12.2 us (4%)
    all_to_all x1, waiting for transfers between devices, body(): lax.all_to_all(split, 'ops', split_axis=2, concat_axis=0, tiled=True)  105 us
    all_to_all x1, waiting for transfers between devices, body(): lax.all_to_all(ordered, 'ops', split_axis=0, concat_axis=2, tiled=True)  58.3 us
    ppermute x1, waiting for transfers between devices, with_halo(): lax.ppermute(lax.slice_in_dim(block, block.shape[dim] - width, None, axis...  18.7 us
    gather x1, local copies, waits for them, and re-layouts, body(): ordered = jnp.take(spread, source, axis=0)  15.6 us
    all_to_all x1, starting transfers between devices, body(): lax.all_to_all(split, 'ops', split_axis=2, concat_axis=0, tiled=True)  13.3 us
    dot_general x1, matrix products, body(): jnp.einsum('psba,psbc->psac', targets, half, preferred_element_type=jnp.f...  12.2 us
    gather x2, local copies, waits for them, and re-layouts, body(): targets = jnp.take(kept_near, target_local.reshape(-1), axis=0)  12 us
    unnamed x17, local copies, waits for them, and re-layouts  9.42 us
  transfers between devices with their start and end apart: 4, of which 3 were waited for; matrix products, arithmetic and copies ran while one was open for 10% of the time, Pallas kernels for 0%

commit v1 on v0

--- a/solution.py
+++ b/solution.py
@@ -41,7 +41,10 @@
     offsets = jnp.take(shift, mine)
     strip = width // ops_count
     split = operators.reshape(pair_dev, sector_dev, ops_count, strip, width)
-    spread = lax.all_to_all(split, "ops", split_axis=2, concat_axis=0, tiled=True)
+    spread = jnp.concatenate(
+        lax.all_to_all(jnp.stack(jnp.split(split, lax.axis_size("ops"), axis=2)), "ops", 0, 0),
+        axis=0,
+    )
     ordered = jnp.take(spread, source, axis=0)
     returned = lax.all_to_all(ordered, "ops", split_axis=0, concat_axis=2, tiled=True)
     blocks = returned.reshape(pair_dev, sector_dev, width, width)

time: 296 us -> 361 us (1.22)
  local copies, waits for them, and re-layouts: 60.1 us -> 124 us
    unnamed x17 -> x82, local copies, waits for them, and re-layouts: 9.42 us -> 80.7 us
    reshape x1 -> x0, local copies, waits for them, and re-layouts: 7.75 us -> none  [body(): split = operators.reshape(pair_dev, sector_dev, ops_count, strip, width)]
  transfers between devices with their start and end apart: 4 -> 4, of which waited for: 3 -> 3; matrix products, arithmetic and copies ran while one was open for 10% -> 8% of each run, Pallas kernels for 0% -> 0%
where the time goes in v1:
time: 361 us; the launch traced here: 359 us
  waiting for transfers between devices  182 us (50%)
  local copies, waits for them, and re-layouts  124 us (34%)
  starting transfers between devices  22.2 us (6%)
  other arithmetic  19.1 us (5%)
  matrix products  12.2 us (3%)
    all_to_all x1, waiting for transfers between devices, body(): lax.all_to_all(jnp.stack(jnp.split(split, lax.axis_size('ops'), axis=2)),...  105 us
    unnamed x82, local copies, waits for them, and re-layouts  80.7 us
    all_to_all x1, waiting for transfers between devices, body(): lax.all_to_all(ordered, 'ops', split_axis=0, concat_axis=2, tiled=True)  58.3 us
    ppermute x1, waiting for transfers between devices, with_halo(): lax.ppermute(lax.slice_in_dim(block, block.shape[dim] - width, None, axis...  18.7 us
    gather x1, local copies, waits for them, and re-layouts, body(): ordered = jnp.take(spread, source, axis=0)  15.6 us
    all_to_all x1, starting transfers between devices, body(): lax.all_to_all(jnp.stack(jnp.split(split, lax.axis_size('ops'), axis=2)),...  13.3 us
    dot_general x1, matrix products, body(): jnp.einsum('psba,psbc->psac', targets, half, preferred_element_type=jnp.f...  12.2 us
    gather x2, local copies, waits for them, and re-layouts, body(): targets = jnp.take(kept_near, target_local.reshape(-1), axis=0)  11.9 us
  transfers between devices with their start and end apart: 4, of which 3 were waited for; matrix products, arithmetic and copies ran while one was open for 8% of the time, Pallas kernels for 0%

profile of v1, /device:TPU:1, one launch (start us, length us, event | category | flops | bytes accessed | tf_op | source)
XLA Modules:
  0.0 359.3 jit_solution(6685287857301843329)
XLA Ops:
  0.0 9.4 %copy.205 = bf16[2,2,768,768]{3,1,2,0:T(2,128)(2,1)} copy(bf16[2,2,768,768]{3,2,1,0:T(8,128)(2,1)} %param.5) | data formatting | bytes 9437184 | tf_op args[0]
  9.4 1.7 constant_dynamic-update-slice_fusion.63
  11.1 1.6 constant_dynamic-update-slice_fusion.62
  12.7 1.6 constant_dynamic-update-slice_fusion.61
  14.2 1.6 constant_dynamic-update-slice_fusion.60
  15.8 1.6 constant_dynamic-update-slice_fusion.59
  17.3 1.6 constant_dynamic-update-slice_fusion.58
  18.9 1.6 constant_dynamic-update-slice_fusion.57
  20.5 1.6 constant_dynamic-update-slice_fusion.56
  22.0 1.6 constant_dynamic-update-slice_fusion.55
  23.6 1.6 constant_dynamic-update-slice_fusion.54
  25.2 1.6 constant_dynamic-update-slice_fusion.53
  26.8 1.6 constant_dynamic-update-slice_fusion.52
  28.3 1.6 constant_dynamic-update-slice_fusion.51
  29.9 1.6 constant_dynamic-update-slice_fusion.50
  31.5 1.6 constant_dynamic-update-slice_fusion.49
  33.0 1.6 constant_dynamic-update-slice_fusion.48
  34.6 1.6 constant_dynamic-update-slice_fusion.47
  36.2 1.6 constant_dynamic-update-slice_fusion.46
  37.7 1.6 constant_dynamic-update-slice_fusion.45
  39.3 1.6 constant_dynamic-update-slice_fusion.44
  40.9 1.6 constant_dynamic-update-slice_fusion.43
  42.4 1.6 constant_dynamic-update-slice_fusion.42
  44.0 1.6 constant_dynamic-update-slice_fusion.41
  45.6 1.6 constant_dynamic-update-slice_fusion.40
  47.1 1.6 constant_dynamic-update-slice_fusion.39
  48.7 1.6 constant_dynamic-update-slice_fusion.38
  50.2 1.5 constant_dynamic-update-slice_fusion.37
  51.8 1.6 constant_dynamic-update-slice_fusion.36
  53.4 1.6 constant_dynamic-update-slice_fusion.35
  54.9 1.6 constant_dynamic-update-slice_fusion.34
  56.5 1.6 constant_dynamic-update-slice_fusion.33
  58.0 1.6 constant_dynamic-update-slice_fusion.32
  59.6 0.7 constant_dynamic-update-slice_fusion.31
  66.4 0.7 constant_dynamic-update-slice_fusion.21
  67.7 0.7 constant_dynamic-update-slice_fusion.19
  69.1 0.7 constant_dynamic-update-slice_fusion.17
  69.8 0.7 constant_dynamic-update-slice_fusion.16
  70.5 0.7 constant_dynamic-update-slice_fusion.15
  72.5 0.7 constant_dynamic-update-slice_fusion.12
  73.9 0.7 constant_dynamic-update-slice_fusion.10
  77.3 0.7 constant_dynamic-update-slice_fusion.5
  78.7 0.7 constant_dynamic-update-slice_fusion.3
  81.4 13.3 %all-to-all-start = ((bf16[64,2,2,1,12,768]{5,2,4,1,3,0:T(2,128)(2,1)}), bf16[64,2,2,1,12,768]{5,2,4,1,3,0:T(2,128)(2,1)}, u32[]{:S(2)}, u32[]{:S(2)}) async-start(bf16[64,2,2,1,12,768]{5,2,4,1,3,0:T(2,128)(2,1)} %constant_dynamic-update-slice_fusion), calls=%async_computation | async-start | bytes 9437184 | tf_op jit(solution)/shard_map/all_to_all | solution.py:45
  94.7 2.5 sort.17
  97.3 104.5 %all-to-all-done = bf16[64,2,2,1,12,768]{5,2,4,1,3,0:T(2,128)(2,1)} async-done(((bf16[64,2,2,1,12,768]{5,2,4,1,3,0:T(2,128)(2,1)}), bf16[64,2,2,1,12,768]{5,2,4,1,3,0:T(2,128)(2,1)}, u32[]{:S(2)}, u32[]{:S(2)}) %all-to-all-start) | async-done | bytes 4718624 | tf_op jit(solution)/shard_map/all_to_all | solution.py:45
  201.8 15.6 %gather_fusion.4 = bf16[128,2,12,768]{3,1,2,0:T(2,128)(2,1)} fusion(bf16[128,2,12,768]{3,1,2,0:T(2,128)(2,1)} %bitcast.70, s32[1024]{0:T(1024)S(1)} %pad_clamp_fusion), kind=kCustom, calls=%fused_computation.4 | custom fusion | bytes 9437696 | tf_op jit(solution)/shard_map/jit(_take)/gather | solution.py:48
  217.4 8.8 %broadcast_select_fusion = bf16[128,2,1,12,768]{4,1,3,2,0:T(2,128)(2,1)} fusion(pred[128]{0:T(512)(128)(4,1)S(1)} %compare_and_fusion, bf16[128,2,12,768]{3,1,2,0:T(2,128)(2,1)} %gather_fusion.4), kind=kLoop, calls=%fused_computation.5 | loop fusion | flops 2359296 | bytes 9437312 | tf_op jit(solution)/shard_map/jit(_take)/select_n | solution.py:48
  226.2 6.1 %all-to-all-start.1 = ((bf16[128,2,1,12,768]{4,1,3,2,0:T(2,128)(2,1)}), bf16[128,2,1,12,768]{4,1,3,2,0:T(2,128)(2,1)}, u32[]{:S(2)}, u32[]{:S(2)}) async-start(bf16[128,2,1,12,768]{4,1,3,2,0:T(2,128)(2,1)} %broadcast_select_fusion), calls=%async_computation.1 | async-start | bytes 9437184 | tf_op jit(solution)/shard_map/all_to_all | solution.py:49
  232.3 1.6 fusion.32
  233.9 1.3 collective-permute-start
  235.2 1.4 collective-permute-start.1
  236.7 1.2 gather_fusion
  237.9 0.7 and_select_fusion.3
  239.3 1.2 gather_fusion.1
  242.4 1.3 compare_and_fusion.2
  243.7 18.7 %collective-permute-done = bf16[1,768,768]{2,1,0:T(8,128)(2,1)S(1)} collective-permute-done((bf16[1,768,768]{2,1,0:T(8,128)(2,1)}, bf16[1,768,768]{2,1,0:T(8,128)(2,1)S(1)}, u32[]{:S(2)}, u32[]{:S(2)}) %collective-permute-start) | collective-permute-done | bytes 1179680 | tf_op jit(solution)/shard_map/ppermute | solution.py:13
  262.5 3.7 %maximum_select_fusion = bf16[4,768,768]{2,1,0:T(8,128)(2,1)} fusion(bf16[1,768,768]{2,1,0:T(8,128)(2,1)} %collective-permute-done.1, bf16[2,768,768]{2,1,0:T(8,128)(2,1)S(1)} %copy-done.3, bf16[1,768,768]{2,1,0:T(8,128)(2,1)S(1)} %collective-permute-done, pred[4,768]{1,0:T(4,128)(4,1)S(1)} %iota_compare_fusion), kind=kLoop, calls=%fused_computation.6 | loop fusion | flops 7077888 | bytes 9440256 | tf_op jit(solution)/shard_map/jit(_where)/select_n | solution.py:37
  266.1 5.3 %gather_fusion.2 = bf16[4,768,768]{2,1,0:T(8,128)(2,1)} fusion(bf16[4,768,768]{2,1,0:T(8,128)(2,1)} %maximum_select_fusion, s32[1024]{0:T(1024)S(1)} %pad_clamp_fusion.2), kind=kCustom, calls=%fused_computation.2 | custom fusion | bytes 9437200 | tf_op jit(solution)/shard_map/jit(_take)/gather | solution.py:55
  271.4 6.6 %copy.204 = bf16[2,2,768,768]{2,3,1,0:T(8,128)(2,1)} copy(bf16[2,2,768,768]{3,2,1,0:T(8,128)(2,1)} %bitcast.406) | data formatting | bytes 9437184 | tf_op jit(solution)/shard_map/jit(_take)/gather | solution.py:55
  278.1 3.0 gather_fusion.3
  281.1 58.3 %all-to-all-done.1 = bf16[128,2,1,12,768]{4,1,3,2,0:T(2,128)(2,1)} async-done(((bf16[128,2,1,12,768]{4,1,3,2,0:T(2,128)(2,1)}), bf16[128,2,1,12,768]{4,1,3,2,0:T(2,128)(2,1)}, u32[]{:S(2)}, u32[]{:S(2)}) %all-to-all-start.1) | async-done | bytes 4718624 | tf_op jit(solution)/shard_map/all_to_all | solution.py:49
  339.4 7.7 %copy.269 = bf16[2,2,64,1,12,768]{5,1,4,2,0,3:T(2,128)(2,1)} copy(bf16[2,2,64,1,12,768]{5,1,4,0,2,3:T(2,128)(2,1)} %bitcast.73) | data formatting | bytes 9437184 | tf_op jit(solution)/shard_map/all_to_all | solution.py:49
  347.2 12.2 %fusion.7 = bf16[2,2,768,768]{3,2,1,0:T(8,128)(2,1)} fusion(bf16[2,2,768,768]{2,3,1,0:T(8,128)(2,1)} %copy.204, pred[2,2]{1,0:T(4,128)(4,1)S(1)} %copy-done.7, bf16[2,2,768,768]{3,1,2,0:T(2,128)(2,1)} %bitcast.471, bf16[2,768,768]{2,1,0:T(8,128)(2,1)S(1)} %gather_fusion.3, pred[2]{0:T(512)(128)(4,1)S(1)} %copy-done.8), kind=kOutput, calls=%fused_computation.14 | convolution fusion | flops 7256014848 | bytes 16515078 | tf_op jit(solution)/shard_map/psba,psbc->psac/dot_general | solution.py:57
  (58 shorter events, 17.6 us)
Async XLA Ops:
  0.0 239.3 %copy-start = (s32[8]{0:T(128)S(1)}, s32[8]{0:T(128)}, u32[]{:S(2)}) copy-start(s32[8]{0:T(128)} %param.9) | copy-start | bytes 100
  9.4 50.2 %copy-start.2 = (bf16[2,2,768,768]{3,1,2,0:T(2,128)(2,1)S(1)}, bf16[2,2,768,768]{3,1,2,0:T(2,128)(2,1)}, u32[]{:S(2)}) copy-start(bf16[2,2,768,768]{3,1,2,0:T(2,128)(2,1)} %copy.205) | copy-start | bytes 14155780
  81.4 13.3 %copy-start.6 = (s32[128]{0:T(128)S(1)}, s32[128]{0:T(128)}, u32[]{:S(2)}) copy-start(s32[128]{0:T(128)} %param.8) | copy-start | bytes 1540
  81.4 120.4 %all-to-all-start = ((bf16[64,2,2,1,12,768]{5,2,4,1,3,0:T(2,128)(2,1)}), bf16[64,2,2,1,12,768]{5,2,4,1,3,0:T(2,128)(2,1)}, u32[]{:S(2)}, u32[]{:S(2)}) async-start(bf16[64,2,2,1,12,768]{5,2,4,1,3,0:T(2,128)(2,1)} %constant_dynamic-update-slice_fusion), calls=%async_computation | async-start | bytes 9437184 | tf_op jit(solution)/shard_map/all_to_all | solution.py:45
  97.2 139.4 %copy-start.5 = (s32[128]{0:T(128)}, s32[128]{0:T(128)S(1)}, u32[]{:S(2)}) copy-start(s32[128]{0:T(128)S(1)} %get-tuple-element.6) | copy-start | bytes 1540
  226.2 6.1 %copy-start.3 = (bf16[2,768,768]{2,1,0:T(8,128)(2,1)S(1)}, bf16[2,768,768]{2,1,0:T(8,128)(2,1)}, u32[]{:S(2)}) copy-start(bf16[2,768,768]{2,1,0:T(8,128)(2,1)} %param.6) | copy-start | bytes 7077892
  226.2 113.3 %all-to-all-start.1 = ((bf16[128,2,1,12,768]{4,1,3,2,0:T(2,128)(2,1)}), bf16[128,2,1,12,768]{4,1,3,2,0:T(2,128)(2,1)}, u32[]{:S(2)}, u32[]{:S(2)}) async-start(bf16[128,2,1,12,768]{4,1,3,2,0:T(2,128)(2,1)} %broadcast_select_fusion), calls=%async_computation.1 | async-start | bytes 9437184 | tf_op jit(solution)/shard_map/all_to_all | solution.py:49
  232.3 4.4 %copy-start.1 = (s32[128]{0:T(128)S(1)}, s32[128]{0:T(128)}, u32[]{:S(2)}) copy-start(s32[128]{0:T(128)} %param.7) | copy-start | bytes 1540
  233.9 28.6 %collective-permute-start = (bf16[1,768,768]{2,1,0:T(8,128)(2,1)}, bf16[1,768,768]{2,1,0:T(8,128)(2,1)S(1)}, u32[]{:S(2)}, u32[]{:S(2)}) collective-permute-start(bf16[1,768,768]{2,1,0:T(8,128)(2,1)} %get-tuple-element.7), channel_id=1, source_target_pairs={{0,1},{1,2},{2,3},{3,0},{4,5},{5,6},{6,7},{7,4},{8,9},{9,10},{10,1... | collective-permute-start | bytes 3538952 | tf_op jit(solution)/shard_map/ppermute | solution.py:13
  235.2 27.3 %collective-permute-start.1 = (bf16[1,768,768]{2,1,0:T(8,128)(2,1)}, bf16[1,768,768]{2,1,0:T(8,128)(2,1)}, u32[]{:S(2)}, u32[]{:S(2)}) collective-permute-start(bf16[1,768,768]{2,1,0:T(8,128)(2,1)} %get-tuple-element.8), channel_id=1, source_target_pairs={{1,0},{2,1},{3,2},{0,3},{5,4},{6,5},{7,6},{4,7},{9,8},{10,9},{11,1... | collective-permute-start | bytes 3538952 | tf_op jit(solution)/shard_map/ppermute | solution.py:16
  238.6 3.1 copy-start.4
  339.4 7.8 %copy-start.7 = (pred[2,2]{1,0:T(4,128)(4,1)S(1)}, pred[2,2]{1,0:T(4,128)(4,1)}, u32[]{:S(2)}) copy-start(pred[2,2]{1,0:T(4,128)(4,1)} %compare_and_fusion.2) | copy-start | bytes 16
  339.4 7.8 %copy-start.8 = (pred[2]{0:T(512)(128)(4,1)S(1)}, pred[2]{0:T(512)(128)(4,1)}, u32[]{:S(2)}) copy-start(pred[2]{0:T(512)(128)(4,1)} %compare_and_fusion.1) | copy-start | bytes 10
